TPU v7x, 32 devices: a whole 2x2x4 slice. The times are simulated.
32 devices in a mesh: fsdp: 8 (over z, x), dp: 4 (over y, core).
Axes of the slice: x: 2, y: 2, z: 4, core: 2. Of those that a mesh axis runs over, the one named last changes fastest.
Arguments:
- features: bfloat16 [8192, 1024], P(('fsdp', 'dp')), may hold values from -6 to 6
- normed: bfloat16 [8192, 4096], P(('fsdp', 'dp')), may hold values from -6 to 6
- relu_mask: int32 [8192, 4096], P(('fsdp', 'dp')), may hold values 0 or 1
- cotangent: bfloat16 [8192, 4096], P(('fsdp', 'dp')), may hold values from -40 to 40
- weight_shard: bfloat16 [1024, 4096], P('fsdp'), may hold values from -0.1875 to 0.1875
- norm_gain: float32 [4096], replicated, may hold values from 0.25 to 1.75
- inverse_deviation: float32 [4096], replicated, may hold values from 0.5 to 3
Outputs:
- grad_input: bfloat16 [8192, 1024], P(('fsdp', 'dp'))
- grad_weight: float32 [1024, 4096], P('fsdp')
- grad_gain: float32 [4096], replicated
- grad_shift: float32 [4096], replicated
All inputs are finite; a program needn't handle non-finite values. No bound on the sum of `relu_mask` on one device may be relied on, other than what follows from the above.
Results may differ from a plain program's by a relative error of at most 0.005.
Values may be sent and summed in bfloat16 or wider, within the bound.
No kernel may reach another device: no remote copies, remote signals or barrier semaphores. Data moves between devices by JAX's collectives and lax.ppermute only.
A program may use at most 128 MiB of HBM per device.

v0:
```python
import math
import jax
import jax.numpy as jnp
from jax import lax
from jax.sharding import PartitionSpec as P


def on_device(features, normed, relu_mask, cotangent, weight_shard, norm_gain, inverse_deviation):
    local_rows = features.shape[0]
    total_rows = local_rows * lax.axis_size("fsdp") * lax.axis_size("dp")
    masked = cotangent.astype(jnp.float32) * relu_mask.astype(jnp.float32)
    normed_f = normed.astype(jnp.float32)
    local_plain = jnp.sum(masked, axis=0)
    local_cross = jnp.sum(masked * normed_f, axis=0)
    sum_plain, sum_cross = lax.psum((local_plain, local_cross), ("fsdp", "dp"))
    norm_grad = (
        inverse_deviation
        * norm_gain
        * (masked - sum_plain / total_rows - normed_f * (sum_cross / total_rows))
    )
    norm_grad = norm_grad.astype(jnp.bfloat16)
    grad_input = lax.dot_general(
        norm_grad,
        lax.all_gather(weight_shard, "fsdp", axis=0, tiled=True),
        (((1,), (1,)), ((), ())),
        preferred_element_type=jnp.float32,
    ).astype(jnp.bfloat16)
    unit_block = lax.all_to_all(norm_grad, "dp", split_axis=1, concat_axis=0, tiled=True)
    unit_term = lax.dot_general(
        lax.all_gather(features, "dp", axis=0, tiled=True),
        unit_block,
        (((0,), (0,)), ((), ())),
        preferred_element_type=jnp.float32,
    )
    owner_part = lax.psum_scatter(unit_term, "fsdp", scatter_dimension=0, tiled=True)
    summed = lax.all_gather(owner_part, "dp", axis=1, tiled=True)
    rescale = 1.0 / math.sqrt(total_rows)
    return (grad_input, summed * rescale, sum_cross * rescale, sum_plain * rescale)


def solution(mesh):
    in_specs = (
        P(("fsdp", "dp"), None),
        P(("fsdp", "dp"), None),
        P(("fsdp", "dp"), None),
        P(("fsdp", "dp"), None),
        P("fsdp", None),
        P(),
        P(),
    )
    out_specs = (P(("fsdp", "dp"), None), P("fsdp", None), P(), P())
    return jax.shard_map(
        on_device, mesh=mesh, in_specs=in_specs, out_specs=out_specs, check_vma=False
    )
```

profile of v0, /device:TPU:0, one launch (start us, length us, event | category | flops | bytes accessed | tf_op | source)
XLA Modules:
  0.0 361.4 jit_solution(14963796621022647305)
XLA Ops:
  7.2 0.0 all-gather.6.cloned.1.call-start
  7.2 0.7 all-gather.6.cloned.1.call-update
  7.9 0.0 reduce-scatter.2.cloned.1.call-start
  7.9 3.3 copy.15
  11.2 5.6 %copy.14 = s32[256,4096]{0,1:T(8,128)} copy(s32[256,4096]{1,0:T(8,128)} %param.9) | data formatting | bytes 8388608 | tf_op args[2]
  16.8 4.1 %copy.13 = bf16[256,4096]{0,1:T(8,128)(2,1)} copy(bf16[256,4096]{1,0:T(8,128)(2,1)} %param.10) | data formatting | bytes 4194304 | tf_op args[3]
  21.0 0.0 copy-start.2
  21.0 0.0 copy-start.3
  21.0 4.1 %fusion.4 = (f32[4096]{0:T(1024)S(1)}, f32[4096]{0:T(1024)S(1)}) fusion(s32[256,4096]{0,1:T(8,128)} %copy.14, bf16[256,4096]{0,1:T(8,128)(2,1)} %copy.13, bf16[256,4096]{0,1:T(8,128)(2,1)S(1)} %copy.15), kind=kLoop, calls=%fused_computation.8 | loop fusion | flops 7331840 | bytes 8421376 | tf_op jit(solution)/shard_map/reduce_sum | solution.py:13
  25.1 0.0 copy-done.2
  25.1 0.0 copy-done.3
  25.1 42.3 %all-reduce = (f32[4096]{0:T(1024)S(1)}, f32[4096]{0:T(1024)S(1)}) all-reduce(f32[4096]{0:T(1024)S(1)} %get-tuple-element.17, f32[4096]{0:T(1024)S(1)} %get-tuple-element.16), channel_id=1, replica_groups=mesh['fsdp'=8,'dp'=4] {'fsdp','dp'}, use_global_device_ids=true, to_apply=%region_3.0 | all-reduce | flops 8192 | bytes 65536 | tf_op jit(solution)/shard_map/psum | solution.py:15
  67.4 0.6 broadcast_multiply_fusion.1
  68.0 4.3 %fusion.3 = bf16[256,4096]{0,1:T(8,128)(2,1)S(1)} fusion(bf16[256,4096]{0,1:T(8,128)(2,1)S(1)} %copy.15, f32[4096]{0:T(1024)S(1)} %get-tuple-element.24, f32[4096]{0:T(1024)S(1)} %get-tuple-element.21, f32[4096]{0:T(1024)S(1)} %mul.37, s32[256,4096]{0,1:T(8,128)} %copy.14, bf16[256,4096]{0,1:T(8,128)(2,1)} %copy.13), kind=kLoop, calls=%fused_computation.5 | loop fusion | flops 9437184 | bytes 10534912 | tf_op jit(solution)/shard_map/convert_element_type | solution.py:21
  72.3 0.0 copy-start
  72.3 29.0 %all_to_all.19 = bf16[256,4,1024]{0,2,1:T(8,128)(2,1)S(1)} all-to-all(bf16[256,4,1024]{0,2,1:T(8,128)(2,1)S(1)} %bitcast.9), channel_id=1, replica_groups=mesh['fsdp'=8,'dp'=4] {'dp'}, dimensions={1} | all-to-all | bytes 4194304 | tf_op jit(solution)/shard_map/all_to_all | solution.py:28
  101.3 0.0 copy-done
  101.3 2.4 copy.16
  103.7 0.0 all-gather.6.cloned.1.call-done
  103.7 6.5 %convolution_bitcast_fusion = f32[1024,1024]{0,1:T(8,128)} fusion(bf16[1024,1024]{1,0:T(8,128)(2,1)} %bitcast.11, bf16[1024,1024]{1,0:T(8,128)(2,1)} %all-gather.6.cloned.1.call-done), kind=kOutput, calls=%fused_computation.7 | convolution fusion | flops 2147483648 | bytes 8388608 | tf_op jit(solution)/shard_map/dot_general | solution.py:29
  110.3 0.0 reduce-scatter.2.cloned.1.call-update
  110.3 0.0 all-gather.8.cloned.1.call-start
  110.3 87.7 %reduce-scatter.2.cloned.1.call-done = f32[128,1024]{0,1:T(8,128)} async-done(((f32[1024,1024]{0,1:T(8,128)}), f32[128,1024]{0,1:T(8,128)}) %reduce-scatter.2.cloned.1.call-update) | async-done | bytes 524304 | tf_op jit(solution)/shard_map/reduce_scatter | solution.py:35
  198.0 0.0 all-gather.8.cloned.1.call-update
  198.1 0.0 all-gather.4.cloned.1.call-start
  198.1 0.5 all-gather.4.cloned.1.call-update
  198.6 23.2 %all-gather.8.cloned.1.call-done = f32[128,4096]{0,1:T(8,128)} async-done(((f32[128,1024]{0,1:T(8,128)}), f32[128,4096]{0,1:T(8,128)}) %all-gather.8.cloned.1.call-update) | async-done | bytes 2097168 | tf_op jit(solution)/shard_map/all_gather | solution.py:36
  221.8 3.1 broadcast_multiply_fusion
  224.9 3.0 copy.17
  227.9 120.4 %all-gather.4.cloned.1.call-done = bf16[1024,4096]{1,0:T(8,128)(2,1)} async-done(((bf16[128,4096]{1,0:T(8,128)(2,1)}), bf16[1024,4096]{1,0:T(8,128)(2,1)}) %all-gather.4.cloned.1.call-update) | async-done | bytes 8388624 | tf_op jit(solution)/shard_map/all_gather | solution.py:24
  348.3 0.0 copy-done.1
  348.3 6.6 %convolution_convert_fusion = bf16[256,1024]{1,0:T(8,128)(2,1)} fusion(bf16[256,4096]{0,1:T(8,128)(2,1)S(1)} %copy-done.1, bf16[1024,4096]{1,0:T(8,128)(2,1)} %all-gather.4.cloned.1.call-done), kind=kOutput, calls=%fused_computation.9 | convolution fusion | flops 2147745792 | bytes 11010048 | tf_op jit(solution)/shard_map/dot_general | solution.py:22
  (2 shorter events, 0.0 us)
Async XLA Ops:
  7.2 96.6 %all-gather.6.cloned.1.call-start = ((), (), s32[]{:S(2)}) async-start(), calls=%async_computation.3 | async-start | bytes 2621440 | tf_op jit(solution)/shard_map/all_gather | solution.py:30
  7.9 190.1 %reduce-scatter.2.cloned.1.call-start = ((), (), s32[]{:S(2)}) async-start(), calls=%async_computation.4 | async-start | bytes 4718592 | tf_op jit(solution)/shard_map/reduce_scatter | solution.py:35
  21.0 4.1 %copy-start.2 = (f32[4096]{0:T(1024)S(1)}, f32[4096]{0:T(1024)}, u32[]{:S(2)}) copy-start(f32[4096]{0:T(1024)} %param.13) | copy-start | bytes 49156
  21.0 4.1 %copy-start.3 = (f32[4096]{0:T(1024)S(1)}, f32[4096]{0:T(1024)}, u32[]{:S(2)}) copy-start(f32[4096]{0:T(1024)} %param.12) | copy-start | bytes 49156
  72.3 29.0 %copy-start = (bf16[256,4096]{0,1:T(8,128)(2,1)}, bf16[256,4096]{0,1:T(8,128)(2,1)S(1)}, u32[]{:S(2)}) copy-start(bf16[256,4096]{0,1:T(8,128)(2,1)S(1)} %fusion.3) | copy-start | bytes 6291460
  110.3 111.5 %all-gather.8.cloned.1.call-start = ((), (), s32[]{:S(2)}) async-start(), calls=%async_computation.5 | async-start | bytes 2621440 | tf_op jit(solution)/shard_map/all_gather | solution.py:36
  198.1 150.2 %all-gather.4.cloned.1.call-start = ((), (), s32[]{:S(2)}) async-start(), calls=%async_computation.2 | async-start | bytes 9437184 | tf_op jit(solution)/shard_map/all_gather | solution.py:24
  224.9 123.4 %copy-start.1 = (bf16[256,4096]{0,1:T(8,128)(2,1)S(1)}, bf16[256,4096]{0,1:T(8,128)(2,1)}, u32[]{:S(2)}) copy-start(bf16[256,4096]{0,1:T(8,128)(2,1)} %copy-done) | copy-start | bytes 6291460
Sparse Core Ops, SparseCore 0:
  9.5 25.2 all-gather.5
  110.4 87.5 reduce-scatter.1
  199.6 22.1 all-gather.7
  223.8 124.4 all-gather.3
where the time goes:
time: 362 us; the launch traced here: 361 us
  waiting for transfers between devices  232 us (64%)
  blocking collectives  71.3 us (20%)
  local copies, waits for them, and re-layouts  18.4 us (5%)
  between operations  13.8 us (4%)
  matrix products  13.1 us (4%)
  other arithmetic  12.1 us (3%)
    all_gather x1, waiting for transfers between devices, on_device(): lax.all_gather(weight_shard, 'fsdp', axis=0, tiled=True)  120 us
    reduce_scatter x1, waiting for transfers between devices, on_device(): lax.psum_scatter(unit_term, 'fsdp', scatter_dimension=0, tiled=True)  87.7 us
    psum x1, blocking collectives, on_device(): sum_plain, sum_cross = lax.psum((local_plain, local_cross), ('fsdp', 'dp'))  42.3 us
    all_to_all x1, blocking collectives, on_device(): lax.all_to_all(norm_grad, 'dp', split_axis=1, concat_axis=0, tiled=True)  29 us
    all_gather x1, waiting for transfers between devices, on_device(): summed = lax.all_gather(owner_part, 'dp', axis=1, tiled=True)  23.2 us
    unnamed x12, local copies, waits for them, and re-layouts  16.1 us
  transfers between devices with their start and end apart: 4, of which 3 were waited for; matrix products, arithmetic and copies ran while one was open for 8% of the time, Pallas kernels for 0%

commit v1 on v0

--- a/solution.py
+++ b/solution.py
@@ -3,6 +3,13 @@
 import jax.numpy as jnp
 from jax import lax
 from jax.sharding import PartitionSpec as P
+
+
+def trade_parts(value, axis, split, join):
+    count = lax.axis_size(axis)
+    pieces = jnp.stack(jnp.split(value, count, axis=split), axis=0)
+    pieces = lax.all_to_all(pieces, axis, split_axis=0, concat_axis=0)
+    return jnp.concatenate(pieces, axis=join)
 
 
 def on_device(features, normed, relu_mask, cotangent, weight_shard, norm_gain, inverse_deviation):
@@ -25,7 +32,7 @@
         (((1,), (1,)), ((), ())),
         preferred_element_type=jnp.float32,
     ).astype(jnp.bfloat16)
-    unit_block = lax.all_to_all(norm_grad, "dp", split_axis=1, concat_axis=0, tiled=True)
+    unit_block = trade_parts(norm_grad, "dp", 1, 0)
     unit_term = lax.dot_general(
         lax.all_gather(features, "dp", axis=0, tiled=True),
         unit_block,

time: 362 us -> 349 us (0.964)
  local copies, waits for them, and re-layouts: 18.4 us -> 3.06 us
    unnamed x12 -> x5, local copies, waits for them, and re-layouts: 16.1 us -> 2.89 us
  transfers between devices with their start and end apart: 4 -> 4, of which waited for: 3 -> 3; matrix products, arithmetic and copies ran while one was open for 8% -> 5% of each run, Pallas kernels for 0% -> 0%
where the time goes in v1:
time: 349 us; the launch traced here: 348 us
  waiting for transfers between devices  233 us (67%)
  blocking collectives  71.7 us (21%)
  between operations  13.8 us (4%)
  other arithmetic  13.1 us (4%)
  matrix products  13.1 us (4%)
    all_gather x1, waiting for transfers between devices, on_device(): lax.all_gather(weight_shard, 'fsdp', axis=0, tiled=True)  120 us
    reduce_scatter x1, waiting for transfers between devices, on_device(): lax.psum_scatter(unit_term, 'fsdp', scatter_dimension=0, tiled=True)  88.5 us
    psum x1, blocking collectives, on_device(): sum_plain, sum_cross = lax.psum((local_plain, local_cross), ('fsdp', 'dp'))  42.6 us
    all_to_all x1, blocking collectives, trade_parts(): pieces = lax.all_to_all(pieces, axis, split_axis=0, concat_axis=0)  29.1 us
    all_gather x1, waiting for transfers between devices, on_device(): summed = lax.all_gather(owner_part, 'dp', axis=1, tiled=True)  23.2 us
  transfers between devices with their start and end apart: 4, of which 3 were waited for; matrix products, arithmetic and copies ran while one was open for 5% of the time, Pallas kernels for 0%

profile of v1, /device:TPU:0, one launch (start us, length us, event | category | flops | bytes accessed | tf_op | source)
XLA Modules:
  0.0 348.4 jit_solution(628145276724356067)
XLA Ops:
  7.2 0.0 all-gather.6.cloned.1.call-start
  7.2 0.7 all-gather.6.cloned.1.call-update
  7.9 0.0 copy-start
  7.9 0.0 copy-start.1
  7.9 0.0 reduce-scatter.2.cloned.1.call-start
  8.0 4.5 %fusion.4 = (f32[4096]{0:T(1024)S(1)}, f32[4096]{0:T(1024)S(1)}) fusion(s32[256,4096]{1,0:T(8,128)} %param.9, bf16[256,4096]{1,0:T(8,128)(2,1)} %param.10, bf16[256,4096]{1,0:T(8,128)(2,1)} %param.8), kind=kLoop, calls=%fused_computation.9 | loop fusion | flops 7331840 | bytes 8421376 | tf_op jit(solution)/shard_map/reduce_sum | solution.py:20
  12.5 42.6 %all-reduce = (f32[4096]{0:T(1024)S(1)}, f32[4096]{0:T(1024)S(1)}) all-reduce(f32[4096]{0:T(1024)S(1)} %get-tuple-element.9, f32[4096]{0:T(1024)S(1)} %get-tuple-element.8), channel_id=1, replica_groups=mesh['fsdp'=8,'dp'=4] {'fsdp','dp'}, use_global_device_ids=true, to_apply=%region_3.0 | all-reduce | flops 8192 | bytes 65536 | tf_op jit(solution)/shard_map/psum | solution.py:22
  55.0 0.6 broadcast_multiply_fusion.1
  55.6 0.0 copy-done
  55.6 0.0 copy-done.1
  55.7 4.7 %fusion.3 = bf16[256,4096]{1,0:T(8,128)(2,1)S(1)} fusion(bf16[256,4096]{1,0:T(8,128)(2,1)} %param.8, f32[4096]{0:T(1024)S(1)} %get-tuple-element.20, f32[4096]{0:T(1024)S(1)} %get-tuple-element.17, f32[4096]{0:T(1024)S(1)} %mul.37, s32[256,4096]{1,0:T(8,128)} %param.9, bf16[256,4096]{1,0:T(8,128)(2,1)} %param.10), kind=kLoop, calls=%fused_computation.5 | loop fusion | flops 9437184 | bytes 10534912 | tf_op jit(solution)/shard_map/convert_element_type | solution.py:28
  60.3 0.2 slice_bitcast_fusion.3
  60.5 0.3 pad_maximum_fusion
  60.8 29.1 %all_to_all.5 = bf16[4,256,1024]{2,1,0:T(8,128)(2,1)} all-to-all(bf16[4,256,1024]{2,1,0:T(8,128)(2,1)S(1)} %pad_maximum_fusion), channel_id=1, replica_groups=mesh['fsdp'=8,'dp'=4] {'dp'}, dimensions={0} | all-to-all | bytes 4194304 | tf_op jit(solution)/shard_map/all_to_all | solution.py:11
  89.9 0.0 all-gather.6.cloned.1.call-done
  89.9 6.5 %convolution_bitcast_fusion = f32[1024,1024]{0,1:T(8,128)} fusion(bf16[1024,1024]{1,0:T(8,128)(2,1)} %bitcast.15, bf16[1024,1024]{1,0:T(8,128)(2,1)} %all-gather.6.cloned.1.call-done), kind=kOutput, calls=%fused_computation.7 | convolution fusion | flops 2147483648 | bytes 8388608 | tf_op jit(solution)/shard_map/dot_general | solution.py:36
  96.5 0.0 reduce-scatter.2.cloned.1.call-update
  96.5 0.0 all-gather.8.cloned.1.call-start
  96.5 88.5 %reduce-scatter.2.cloned.1.call-done = f32[128,1024]{0,1:T(8,128)} async-done(((f32[1024,1024]{0,1:T(8,128)}), f32[128,1024]{0,1:T(8,128)}) %reduce-scatter.2.cloned.1.call-update) | async-done | bytes 524304 | tf_op jit(solution)/shard_map/reduce_scatter | solution.py:42
  185.0 0.0 all-gather.8.cloned.1.call-update
  185.0 0.0 all-gather.4.cloned.1.call-start
  185.1 0.5 all-gather.4.cloned.1.call-update
  185.6 23.2 %all-gather.8.cloned.1.call-done = f32[128,4096]{0,1:T(8,128)} async-done(((f32[128,1024]{0,1:T(8,128)}), f32[128,4096]{0,1:T(8,128)}) %all-gather.8.cloned.1.call-update) | async-done | bytes 2097168 | tf_op jit(solution)/shard_map/all_gather | solution.py:43
  208.8 3.1 broadcast_multiply_fusion
  211.9 2.9 copy.11
  214.8 120.5 %all-gather.4.cloned.1.call-done = bf16[1024,4096]{1,0:T(8,128)(2,1)} async-done(((bf16[128,4096]{1,0:T(8,128)(2,1)}), bf16[1024,4096]{1,0:T(8,128)(2,1)}) %all-gather.4.cloned.1.call-update) | async-done | bytes 8388624 | tf_op jit(solution)/shard_map/all_gather | solution.py:31
  335.3 6.5 %convolution_convert_fusion = bf16[256,1024]{1,0:T(8,128)(2,1)} fusion(bf16[256,4096]{1,0:T(8,128)(2,1)S(1)} %fusion.3, bf16[1024,4096]{1,0:T(8,128)(2,1)} %all-gather.4.cloned.1.call-done), kind=kOutput, calls=%fused_computation.10 | convolution fusion | flops 2147745792 | bytes 11010048 | tf_op jit(solution)/shard_map/dot_general | solution.py:29
  (1 shorter events, 0.0 us)
Async XLA Ops:
  7.2 82.8 %all-gather.6.cloned.1.call-start = ((), (), s32[]{:S(2)}) async-start(), calls=%async_computation.3 | async-start | bytes 2621440 | tf_op jit(solution)/shard_map/all_gather | solution.py:37
  7.9 47.7 %copy-start = (f32[4096]{0:T(1024)S(1)}, f32[4096]{0:T(1024)}, u32[]{:S(2)}) copy-start(f32[4096]{0:T(1024)} %param.13) | copy-start | bytes 49156
  7.9 47.7 %copy-start.1 = (f32[4096]{0:T(1024)S(1)}, f32[4096]{0:T(1024)}, u32[]{:S(2)}) copy-start(f32[4096]{0:T(1024)} %param.12) | copy-start | bytes 49156
  7.9 177.1 %reduce-scatter.2.cloned.1.call-start = ((), (), s32[]{:S(2)}) async-start(), calls=%async_computation.4 | async-start | bytes 4718592 | tf_op jit(solution)/shard_map/reduce_scatter | solution.py:42
  96.5 112.3 %all-gather.8.cloned.1.call-start = ((), (), s32[]{:S(2)}) async-start(), calls=%async_computation.5 | async-start | bytes 2621440 | tf_op jit(solution)/shard_map/all_gather | solution.py:43
  185.0 150.3 %all-gather.4.cloned.1.call-start = ((), (), s32[]{:S(2)}) async-start(), calls=%async_computation.2 | async-start | bytes 9437184 | tf_op jit(solution)/shard_map/all_gather | solution.py:31
Sparse Core Ops, SparseCore 0:
  9.5 25.8 all-gather.5
  96.6 88.3 reduce-scatter.1
  186.6 22.1 all-gather.7
  210.8 124.4 all-gather.3
